TPU v7x, 256 devices: a whole 4x4x8 slice. The times are simulated.
256 devices in a mesh: section: 2 (over core), dp: 8 (over y_hi, x), tensor: 16 (over z, y_lo).
Axes of the slice: x: 4, y: 4 (y_hi: 2, y_lo: 2; y = y_hi * 2 + y_lo), z: 8, core: 2. Of those that a mesh axis runs over, the one named last changes fastest.
Arguments:
- tokens_in: bfloat16 [1024, 8192], P('dp', ('section', 'tensor')), may hold values from -70 to 70
- gain_attn: bfloat16 [8192], replicated, may hold values from 0.5 to 1.5
- w_query: bfloat16 [8192, 8192], P(None, ('section', 'tensor')), may hold values from -6 to 6
- w_keyval: bfloat16 [8192, 2048], P(None, ('section', 'tensor')), may hold values from -0.0625 to 0.0625
- w_out: bfloat16 [8192, 8192], P(('section', 'tensor')), may hold values from -0.0625 to 0.0625
- gain_mlp: bfloat16 [8192], replicated, may hold values from 0.5 to 1.5
- w_gate: bfloat16 [8192, 16384], P('dp', ('section', 'tensor')), may hold values from -0.0625 to 0.0625
- w_up: bfloat16 [8192, 16384], P('dp', ('section', 'tensor')), may hold values from -0.0625 to 0.0625
- w_down: bfloat16 [16384, 8192], P(('section', 'tensor'), 'dp'), may hold values from -0.046875 to 0.046875
Outputs:
- layer_out: bfloat16 [1024, 8192], P(('section', 'tensor'), 'dp')
All inputs are finite; a program needn't handle non-finite values.
Results may differ from a plain program's by a relative error of at most 0.0068.
Values may be sent and summed in bfloat16 or wider, within the bound.
No kernel may reach another device: no remote copies, remote signals or barrier semaphores. Data moves between devices by JAX's collectives and lax.ppermute only.
A program may use at most 64 MiB of HBM per device.

v0:
```python
import jax
import jax.numpy as jnp
from jax import lax
from jax.sharding import PartitionSpec as P

H = 64
KVH = 8
HD = 128


EPS = 1e-05
THETA = 10000.0


def copy_for_each(array, axis):
    length = lax.axis_size(axis)
    return lax.all_to_all(
        jnp.broadcast_to(array[None], (length, *array.shape)), axis, 0, 0, tiled=True
    )


def in_order(tiles, dim):
    tiles = jnp.moveaxis(tiles, 0, dim)
    dims = tiles.shape
    return tiles.reshape(*dims[:dim], dims[dim] * dims[dim + 1], *dims[dim + 2 :])


def gather_directly(array, axis, dim):
    tiles = copy_for_each(array, axis)
    return in_order(tiles, dim)


def in_blocks(array, dim, length):
    dims = array.shape
    tiles = array.reshape(*dims[:dim], length, dims[dim] // length, *dims[dim + 1 :])
    return jnp.moveaxis(tiles, dim, 0)


def sent_and_summed(array, axis, dim):
    tiles = in_blocks(array, dim, lax.axis_size(axis))
    arrived = lax.all_to_all(tiles, axis, split_axis=0, concat_axis=0, tiled=True)
    return arrived.astype(jnp.float32).sum(axis=0)


def rms_scale(row_data, gain_row):
    values = row_data.astype(jnp.float32)
    factor = lax.rsqrt(jnp.mean(values * values, axis=-1, keepdims=True) + EPS)
    return (values * factor * gain_row.astype(jnp.float32)).astype(jnp.bfloat16)


def rotary(values, positions):
    half_dim = values.shape[-1] // 2
    frequency = THETA ** (-jnp.arange(half_dim, dtype=jnp.float32) * 2.0 / values.shape[-1])
    angles = positions.astype(jnp.float32)[:, None] * frequency[None, :]
    cosine = jnp.cos(angles)[:, None, :]
    sine_part = jnp.sin(angles)[:, None, :]
    first_half = values[..., :half_dim]
    second = values[..., half_dim:]
    return jnp.concatenate(
        [first_half * cosine - second * sine_part, second * cosine + first_half * sine_part],
        axis=-1,
    )


def shards(tokens_in, gain_attn, w_query, w_keyval, w_out, gain_mlp, w_gate, w_up, w_down):
    group_count = lax.axis_size(("section", "tensor"))
    group_index = lax.axis_index(("section", "tensor"))
    data_index = lax.axis_index("dp")
    local_rows = tokens_in.shape[0]
    full_rows = lax.all_gather(tokens_in, ("section", "tensor"), axis=1, tiled=True)
    normed_attn = rms_scale(full_rows, gain_attn)
    heads_dev = w_query.shape[1] // HD
    group_size = H // KVH
    kv_dev = max(1, heads_dev // group_size)
    positions_local = data_index * local_rows + jnp.arange(local_rows, dtype=jnp.int32)
    query_proj = jnp.dot(normed_attn, w_query, preferred_element_type=jnp.float32)
    query_rot = rotary(query_proj.reshape(local_rows, heads_dev, HD), positions_local).astype(
        jnp.bfloat16
    )
    keyval_part = jnp.dot(normed_attn, w_keyval, preferred_element_type=jnp.float32).astype(
        jnp.bfloat16
    )
    keyval_rows = gather_directly(keyval_part, ("section", "tensor"), 1)
    first_kv = group_index * heads_dev // group_size
    key_cols = lax.dynamic_slice_in_dim(keyval_rows, first_kv * HD, kv_dev * HD, 1)
    value_cols = lax.dynamic_slice_in_dim(keyval_rows, KVH * HD + first_kv * HD, kv_dev * HD, 1)
    needed = jnp.concatenate([key_cols, value_cols], axis=1)
    kv_all = gather_directly(needed, "dp", 0)
    total_rows = kv_all.shape[0]
    key_pos = jnp.arange(total_rows, dtype=jnp.int32)
    key_rot = rotary(
        kv_all[:, : kv_dev * HD].astype(jnp.float32).reshape(total_rows, kv_dev, HD), key_pos
    ).astype(jnp.bfloat16)
    value_all = kv_all[:, kv_dev * HD :].reshape(total_rows, kv_dev, HD)
    query_grp = query_rot.reshape(local_rows, kv_dev, heads_dev // kv_dev, HD)
    scores = jnp.einsum(
        "rkgd,skd->kgrs", query_grp, key_rot, preferred_element_type=jnp.float32
    ) * HD ** (-0.5)
    allowed = key_pos[None, :] <= positions_local[:, None]
    scores = jnp.where(allowed[None, None, :, :], scores, -1e30)
    row_peak = jnp.max(scores, axis=-1, keepdims=True)
    expo_rows = jnp.exp(scores - row_peak)
    prob_rows = (expo_rows / jnp.sum(expo_rows, axis=-1, keepdims=True)).astype(jnp.bfloat16)
    attended = jnp.einsum(
        "kgrs,skd->rkgd", prob_rows, value_all, preferred_element_type=jnp.float32
    )
    attended = attended.astype(jnp.bfloat16).reshape(local_rows, heads_dev * HD)
    head_terms = jnp.dot(attended, w_out, preferred_element_type=jnp.float32)
    shared = sent_and_summed(head_terms.astype(jnp.bfloat16), ("section", "tensor"), 1)
    mid_part = (tokens_in.astype(jnp.float32) + shared).astype(jnp.bfloat16)
    mid_full = lax.all_gather(mid_part, ("section", "tensor"), axis=1, tiled=True)
    mid_values = mid_full.astype(jnp.float32)
    row_factor = lax.rsqrt(jnp.mean(mid_values * mid_values, axis=-1, keepdims=True) + EPS)
    mid_cols = lax.all_to_all(mid_full, "dp", split_axis=1, concat_axis=0, tiled=True)
    factor_all = gather_directly(row_factor, "dp", 0)
    block_width = mid_cols.shape[1]
    gain_cols = lax.dynamic_slice_in_dim(gain_mlp, data_index * block_width, block_width, 0)
    norm_cols = (
        mid_cols.astype(jnp.float32) * factor_all * gain_cols.astype(jnp.float32)[None, :]
    ).astype(jnp.bfloat16)
    hidden_width = w_gate.shape[1]
    row_block = norm_cols
    gate_block = jnp.dot(row_block, w_gate, preferred_element_type=jnp.float32)
    up_block = jnp.dot(row_block, w_up, preferred_element_type=jnp.float32)
    gate_both = lax.psum_scatter(
        jnp.concatenate([gate_block, up_block], axis=1), "dp", scatter_dimension=0, tiled=True
    )
    hidden_part = (jax.nn.silu(gate_both[:, :hidden_width]) * gate_both[:, hidden_width:]).astype(
        jnp.bfloat16
    )
    hidden_all = gather_directly(hidden_part, "dp", 0)
    out_rows = hidden_all.shape[0] // group_count
    row_block = hidden_all
    down_part = sent_and_summed(
        jnp.dot(row_block, w_down, preferred_element_type=jnp.float32).astype(jnp.bfloat16),
        ("section", "tensor"),
        0,
    )
    resid_rows = lax.dynamic_slice_in_dim(mid_cols, group_index * out_rows, out_rows, 0)
    return (resid_rows.astype(jnp.float32) + down_part).astype(jnp.bfloat16)


def solution(mesh):
    placed = (
        P("dp", ("section", "tensor")),
        P(),
        P(None, ("section", "tensor")),
        P(None, ("section", "tensor")),
        P(("section", "tensor"), None),
        P(),
        P("dp", ("section", "tensor")),
        P("dp", ("section", "tensor")),
        P(("section", "tensor"), "dp"),
    )
    return jax.shard_map(
        shards,
        mesh=mesh,
        in_specs=placed,
        out_specs=P(("section", "tensor"), "dp"),
        check_vma=False,
    )
```

profile of v0, /device:TPU:1, one launch (start us, length us, event | category | flops | bytes accessed | tf_op | source)
XLA Modules:
  0.0 477.5 jit_solution(13598116325704547654)
XLA Ops:
  8.0 70.4 %all-gather.3.cloned.1.call-done = bf16[128,8192]{1,0:T(8,128)(2,1)} async-done(((bf16[128,256]{1,0:T(8,128)(2,1)}), bf16[128,8192]{1,0:T(8,128)(2,1)}) %all-gather.3.cloned.1.call-update) | async-done | bytes 2097168 | tf_op jit(solution)/shard_map/all_gather | solution.py:70
  78.5 2.2 fusion
  80.7 2.8 convolution_convert_fusion.3
  84.4 5.4 %all-to-all-start = ((bf16[32,128,64]{1,2,0:T(8,128)(2,1)}), bf16[32,128,64]{1,2,0:T(8,128)(2,1)}, u32[]{:S(2)}, u32[]{:S(2)}) async-start(bf16[32,128,64]{1,2,0:T(8,128)(2,1)} %broadcast_in_dim.16), calls=%async_computation | async-start | bytes 1048576 | tf_op jit(solution)/shard_map/all_to_all | solution.py:17
  90.3 3.0 fusion.12
  93.4 13.7 %all-to-all-done = bf16[32,128,64]{1,2,0:T(8,128)(2,1)} async-done(((bf16[32,128,64]{1,2,0:T(8,128)(2,1)}), bf16[32,128,64]{1,2,0:T(8,128)(2,1)}, u32[]{:S(2)}, u32[]{:S(2)}) %all-to-all-start) | async-done | bytes 524320 | tf_op jit(solution)/shard_map/all_to_all | solution.py:17
  108.8 6.4 %all-to-all-start.1 = ((bf16[8,128,256]{2,1,0:T(8,128)(2,1)}), bf16[8,128,256]{2,1,0:T(8,128)(2,1)S(1)}, u32[]{:S(2)}, u32[]{:S(2)}) async-start(bf16[8,128,256]{2,1,0:T(8,128)(2,1)} %broadcast_in_dim.17), calls=%async_computation.1 | async-start | bytes 1048576 | tf_op jit(solution)/shard_map/all_to_all | solution.py:17
  115.5 11.7 %all-to-all-done.1 = bf16[8,128,256]{2,1,0:T(8,128)(2,1)S(1)} async-done(((bf16[8,128,256]{2,1,0:T(8,128)(2,1)}), bf16[8,128,256]{2,1,0:T(8,128)(2,1)S(1)}, u32[]{:S(2)}, u32[]{:S(2)}) %all-to-all-start.1) | async-done | bytes 524320 | tf_op jit(solution)/shard_map/all_to_all | solution.py:17
  127.2 2.4 fusion.25
  131.7 54.1 %all_to_all.49 = bf16[32,128,256]{2,1,0:T(8,128)(2,1)S(1)} all-to-all(bf16[32,128,256]{2,1,0:T(8,128)(2,1)S(1)} %bitcast.62), channel_id=1, replica_groups=mesh['section'=2,'dp'=8,'tensor'=16] {'section','tensor'}, dimensions={0} | all-to-all | bytes 4194304 | tf_op jit(solution)/shard_map/all_to_all | solution.py:41
  186.7 59.9 %all-gather.5.cloned.1.call-done = bf16[128,8192]{1,0:T(8,128)(2,1)} async-done(((bf16[128,256]{1,0:T(8,128)(2,1)}), bf16[128,8192]{1,0:T(8,128)(2,1)}) %all-gather.5.cloned.1.call-update) | async-done | bytes 2097168 | tf_op jit(solution)/shard_map/all_gather | solution.py:111
  246.6 2.1 multiply_reduce_fusion
  249.3 6.5 %all-to-all-start.4 = ((f32[8,128,1]{1,2,0:T(1,128)}), f32[8,128,1]{1,2,0:T(1,128)S(1)}, u32[]{:S(2)}, u32[]{:S(2)}) async-start(f32[8,128,1]{1,2,0:T(1,128)} %broadcast_in_dim.20), calls=%async_computation.4 | async-start | bytes 8192 | tf_op jit(solution)/shard_map/all_to_all | solution.py:17
  255.8 3.1 copy.45
  259.0 3.3 all-to-all-done.4
  262.3 3.6 all-to-all-start.3
  266.6 27.8 %all-to-all-done.3 = bf16[128,8,1024]{2,0,1:T(8,128)(2,1)S(1)} async-done(((bf16[128,8,1024]{2,0,1:T(8,128)(2,1)}), bf16[128,8,1024]{2,0,1:T(8,128)(2,1)S(1)}, u32[]{:S(2)}, u32[]{:S(2)}) %all-to-all-start.3) | async-done | bytes 2097184 | tf_op jit(solution)/shard_map/all_to_all | solution.py:114
  294.4 3.4 fusion.10
  299.3 2.5 pad_maximum_fusion
  301.8 84.1 %reduce-scatter.2.cloned.1.call-done = f32[128,1024]{0,1:T(8,128)} async-done(((f32[1024,1024]{0,1:T(8,128)}), f32[128,1024]{0,1:T(8,128)}) %reduce-scatter.2.cloned.1.call-update) | async-done | bytes 524304 | tf_op jit(solution)/shard_map/reduce_scatter | solution.py:125
  387.2 17.7 %all_to_all.50 = bf16[8,128,512]{2,1,0:T(8,128)(2,1)S(1)} all-to-all(bf16[8,128,512]{2,1,0:T(8,128)(2,1)S(1)} %broadcast_in_dim.21), channel_id=1, replica_groups=mesh['section'=2,'dp'=8,'tensor'=16] {'dp'}, dimensions={0} | all-to-all | bytes 2097152 | tf_op jit(solution)/shard_map/all_to_all | solution.py:17
  405.0 2.6 convolution_convert_fusion.1
  407.6 11.5 %all-to-all-start.6 = ((bf16[32,32,1024]{2,1,0:T(8,128)(2,1)}), bf16[32,32,1024]{2,1,0:T(8,128)(2,1)S(1)}, u32[]{:S(2)}, u32[]{:S(2)}) async-start(bf16[32,32,1024]{2,1,0:T(8,128)(2,1)} %bitcast.66), calls=%async_computation.7 | async-start | bytes 4194304 | tf_op jit(solution)/shard_map/all_to_all | solution.py:41
  419.1 50.0 %all-to-all-done.6 = bf16[32,32,1024]{2,1,0:T(8,128)(2,1)S(1)} async-done(((bf16[32,32,1024]{2,1,0:T(8,128)(2,1)}), bf16[32,32,1024]{2,1,0:T(8,128)(2,1)S(1)}, u32[]{:S(2)}, u32[]{:S(2)}) %all-to-all-start.6) | async-done | bytes 2097184 | tf_op jit(solution)/shard_map/all_to_all | solution.py:41
  (52 shorter events, 13.8 us)
Async XLA Ops:
  6.5 398.4 %copy-start = (bf16[512,1024]{1,0:T(8,128)(2,1)S(1)}, bf16[512,1024]{1,0:T(8,128)(2,1)}, u32[]{:S(2)}) copy-start(bf16[512,1024]{1,0:T(8,128)(2,1)} %param.17) | copy-start | bytes 3145732
  6.5 71.9 %all-gather.3.cloned.1.call-start = ((), (), s32[]{:S(2)}) async-start(), calls=%async_computation.8 | async-start | bytes 2162688 | tf_op jit(solution)/shard_map/all_gather | solution.py:70
  8.0 81.9 %copy-start.5 = (f32[8192]{0:T(1024)}, f32[8192]{0:T(1024)S(1)}, u32[]{:S(2)}) copy-start(f32[8192]{0:T(1024)S(1)} %convert_element_type.93) | copy-start | bytes 98308
  78.5 11.8 %copy-start.3 = (bf16[128,8192]{1,0:T(8,128)(2,1)S(1)}, bf16[128,8192]{1,0:T(8,128)(2,1)}, u32[]{:S(2)}) copy-start(bf16[128,8192]{1,0:T(8,128)(2,1)} %all-gather.3.cloned.1.call-done) | copy-start | bytes 6291460
  84.4 22.6 %all-to-all-start = ((bf16[32,128,64]{1,2,0:T(8,128)(2,1)}), bf16[32,128,64]{1,2,0:T(8,128)(2,1)}, u32[]{:S(2)}, u32[]{:S(2)}) async-start(bf16[32,128,64]{1,2,0:T(8,128)(2,1)} %broadcast_in_dim.16), calls=%async_computation | async-start | bytes 1048576 | tf_op jit(solution)/shard_map/all_to_all | solution.py:17
  108.8 18.4 %all-to-all-start.1 = ((bf16[8,128,256]{2,1,0:T(8,128)(2,1)}), bf16[8,128,256]{2,1,0:T(8,128)(2,1)S(1)}, u32[]{:S(2)}, u32[]{:S(2)}) async-start(bf16[8,128,256]{2,1,0:T(8,128)(2,1)} %broadcast_in_dim.17), calls=%async_computation.1 | async-start | bytes 1048576 | tf_op jit(solution)/shard_map/all_to_all | solution.py:17
  115.2 131.4 %all-gather.5.cloned.1.call-start = ((), (), s32[]{:S(2)}) async-start(), calls=%async_computation.9 | async-start | bytes 2162688 | tf_op jit(solution)/shard_map/all_gather | solution.py:111
  127.2 3.4 copy-start.1
  131.7 54.4 %copy-start.4 = (bf16[128,256]{1,0:T(8,128)(2,1)S(1)}, bf16[128,256]{1,0:T(8,128)(2,1)}, u32[]{:S(2)}) copy-start(bf16[128,256]{1,0:T(8,128)(2,1)} %param.9) | copy-start | bytes 196612
  249.3 13.0 %all-to-all-start.4 = ((f32[8,128,1]{1,2,0:T(1,128)}), f32[8,128,1]{1,2,0:T(1,128)S(1)}, u32[]{:S(2)}, u32[]{:S(2)}) async-start(f32[8,128,1]{1,2,0:T(1,128)} %broadcast_in_dim.20), calls=%async_computation.4 | async-start | bytes 8192 | tf_op jit(solution)/shard_map/all_to_all | solution.py:17
  262.3 32.2 %all-to-all-start.3 = ((bf16[128,8,1024]{2,0,1:T(8,128)(2,1)}), bf16[128,8,1024]{2,0,1:T(8,128)(2,1)S(1)}, u32[]{:S(2)}, u32[]{:S(2)}) async-start(bf16[128,8,1024]{2,0,1:T(8,128)(2,1)} %bitcast.57), calls=%async_computation.3 | async-start | bytes 4194304 | tf_op jit(solution)/shard_map/all_to_all | solution.py:114
  265.9 120.0 %reduce-scatter.2.cloned.1.call-start = ((), (), s32[]{:S(2)}) async-start(), calls=%async_computation.10 | async-start | bytes 4718592 | tf_op jit(solution)/shard_map/reduce_scatter | solution.py:125
  294.4 4.9 %copy-start.2 = (bf16[128,8,1024]{2,0,1:T(8,128)(2,1)}, bf16[128,8,1024]{2,0,1:T(8,128)(2,1)S(1)}, u32[]{:S(2)}) copy-start(bf16[128,8,1024]{2,0,1:T(8,128)(2,1)S(1)} %all-to-all-done.3) | copy-start | bytes 6291460
  294.4 3.4 copy-start.6
  407.6 61.6 %all-to-all-start.6 = ((bf16[32,32,1024]{2,1,0:T(8,128)(2,1)}), bf16[32,32,1024]{2,1,0:T(8,128)(2,1)S(1)}, u32[]{:S(2)}, u32[]{:S(2)}) async-start(bf16[32,32,1024]{2,1,0:T(8,128)(2,1)} %bitcast.66), calls=%async_computation.7 | async-start | bytes 4194304 | tf_op jit(solution)/shard_map/all_to_all | solution.py:41
Sparse Core Ops, SparseCore 0:
  9.1 69.3 all-gather.2
  186.9 59.7 all-gather.4
  302.0 83.9 reduce-scatter.1
where the time goes:
time: 478 us
  waiting for transfers between devices  322 us (67%)
  blocking collectives  71.8 us (15%)
  starting transfers between devices  33.6 us (7%)
  other arithmetic  15.2 us (3%)
  matrix products  14.8 us (3%)
  between operations  13.4 us (3%)
  local copies, waits for them, and re-layouts  7.15 us (1%)
    reduce_scatter x1, waiting for transfers between devices, shards(): lax.psum_scatter(jnp.concatenate([gate_block, up_block], axis=1), 'dp', s...  84.1 us
    all_gather x1, waiting for transfers between devices, shards(): lax.all_gather(tokens_in, ('section', 'tensor'), axis=1, tiled=True)  70.4 us
    all_gather x1, waiting for transfers between devices, shards(): lax.all_gather(mid_part, ('section', 'tensor'), axis=1, tiled=True)  59.9 us
    all_to_all x1, blocking collectives, sent_and_summed(): lax.all_to_all(tiles, axis, split_axis=0, concat_axis=0, tiled=True)  54.1 us
    all_to_all x1, waiting for transfers between devices, sent_and_summed(): lax.all_to_all(tiles, axis, split_axis=0, concat_axis=0, tiled=True)  50 us
    all_to_all x3, waiting for transfers between devices, copy_for_each(): lax.all_to_all(jnp.broadcast_to(array[None], (length, *array.shape)), axi...  28.7 us
    all_to_all x1, waiting for transfers between devices, shards(): lax.all_to_all(mid_full, 'dp', split_axis=1, concat_axis=0, tiled=True)  27.8 us
    all_to_all x3, starting transfers between devices, copy_for_each(): lax.all_to_all(jnp.broadcast_to(array[None], (length, *array.shape)), axi...  18.3 us
  transfers between devices with their start and end apart: 8, of which 8 were waited for; matrix products, arithmetic and copies ran while one was open for 2% of the time, Pallas kernels for 0%

commit v1 on v0

v1 whole, which is shorter than its diff:
```python
import jax
import jax.numpy as jnp
from jax import lax
from jax.sharding import Mesh
from jax.sharding import PartitionSpec as P

H = 64
KVH = 8
HD = 128
EPS = 1e-05
THETA = 10000.0

F32 = jnp.float32
BF16 = jnp.bfloat16
DP = ("yh", "x")
Z = ("zh", "zl")
GROUP = ("c", "zh", "zl", "yl")
SWAP = [(0, 1), (1, 0)]


def dot(a, b):
    return jnp.dot(a, b, preferred_element_type=F32)


def to_all(array, axis):
    length = lax.axis_size(axis)
    return lax.all_to_all(
        jnp.broadcast_to(array[None], (length, *array.shape)), axis, 0, 0, tiled=True
    )


def exchange(tiles, axis):
    return lax.all_to_all(tiles, axis, 0, 0, tiled=True)


def rope_tables(positions):
    half = HD // 2
    frequency = THETA ** (-jnp.arange(half, dtype=F32) * 2.0 / HD)
    angles = positions.astype(F32)[:, None] * frequency[None, :]
    return jnp.cos(angles), jnp.sin(angles)


def shards(tokens_in, gain_attn, w_query, w_keyval, w_out, gain_mlp, w_gate, w_up, w_down):
    core = lax.axis_index("c")
    block = lax.axis_index(DP)
    z_lo = lax.axis_index("zl")
    y_lo = lax.axis_index("yl")
    rows, width = tokens_in.shape
    n_dp = lax.axis_size(DP)
    n_z = lax.axis_size(Z)
    half_d = w_query.shape[0] // 2
    total = rows * n_dp

    pair = to_all(tokens_in, "yl")
    own = to_all(pair, Z).reshape(2 * n_z, rows, width)
    other = lax.ppermute(own, "c", SWAP)

    def flat(pieces):
        return jnp.moveaxis(pieces, 0, 1).reshape(rows, half_d)

    own_rows, other_rows = flat(own), flat(other)
    parts = ((own_rows, core), (other_rows, 1 - core))
    square = sum(jnp.sum(jnp.square(r.astype(F32)), axis=-1, keepdims=True) for r, _ in parts)
    factor = lax.rsqrt(square / (2 * half_d) + EPS)

    def project(weight):
        out = 0.0
        for r, k in parts:
            gain = lax.dynamic_slice_in_dim(gain_attn, k * half_d, half_d, 0)
            normed = (r.astype(F32) * factor * gain.astype(F32)[None, :]).astype(BF16)
            out = out + dot(normed, lax.dynamic_slice_in_dim(weight, k * half_d, half_d, 0))
        return out

    kv_part = project(w_keyval).astype(BF16).T
    n_group = lax.axis_size(GROUP)
    moves = []
    for g in range(n_group):
        c, z, y = g // (2 * n_z), (g // 2) % n_z, g % 2
        moves.append((g, (z // 4) * 2 * n_z + (2 * (z % 4) + c) * 2 + y))
    kv_here = lax.ppermute(kv_part, GROUP, moves)
    kv_all = to_all(kv_here, ("yh", "x", "zl", "yl")).reshape(n_dp, 2, HD, rows)
    key_t = jnp.moveaxis(kv_all[:, 0], 0, 1).reshape(HD, total)
    value_t = jnp.moveaxis(kv_all[:, 1], 0, 1).reshape(HD, total)
    key_pos = jnp.arange(total, dtype=jnp.int32)
    cos_k, sin_k = rope_tables(key_pos)
    cos_k, sin_k = cos_k.T, sin_k.T
    k1, k2 = key_t[: HD // 2].astype(F32), key_t[HD // 2 :].astype(F32)
    key_rot = jnp.concatenate(
        [k1 * cos_k - k2 * sin_k, k2 * cos_k + k1 * sin_k], axis=0
    ).astype(BF16)

    pos = block * rows + jnp.arange(rows, dtype=jnp.int32)
    cos_q, sin_q = rope_tables(pos)
    query = project(w_query)
    heads = w_query.shape[1] // HD
    q_rot = []
    for h in range(heads):
        q1 = query[:, h * HD : h * HD + HD // 2]
        q2 = query[:, h * HD + HD // 2 : (h + 1) * HD]
        q_rot.append(
            jnp.concatenate([q1 * cos_q - q2 * sin_q, q2 * cos_q + q1 * sin_q], axis=1)
        )
    q_rot = jnp.concatenate(q_rot, axis=0).astype(BF16)
    scores = dot(q_rot, key_rot) * HD ** (-0.5)
    allowed = key_pos[None, :] <= jnp.tile(pos, heads)[:, None]
    scores = jnp.where(allowed, scores, -1e30)
    expo = jnp.exp(scores - jnp.max(scores, axis=-1, keepdims=True))
    probs = (expo / jnp.sum(expo, axis=-1, keepdims=True)).astype(BF16)
    attended = lax.dot_general(
        probs, value_t, (((1,), (1,)), ((), ())), preferred_element_type=F32
    ).astype(BF16)
    attended = jnp.concatenate([attended[h * rows : (h + 1) * rows] for h in range(heads)], axis=1)

    def out_half(k):
        return dot(attended, lax.dynamic_slice_in_dim(w_out, k * half_d, half_d, 1))

    sent = lax.ppermute(out_half(1 - core).astype(BF16), "c", SWAP)
    terms = (out_half(core) + sent.astype(F32)).astype(BF16)
    block_d = half_d // 4
    tiles = terms.reshape(2, rows // 2, 4, block_d).transpose(2, 0, 1, 3)
    tiles = exchange(tiles.reshape(n_z, rows // 2, block_d), Z)
    terms = tiles.astype(F32).sum(axis=0).astype(BF16)
    tiles = exchange(terms.reshape(2, rows // 4, block_d), "yl")
    z_hi = lax.axis_index("zh")
    resid = lax.dynamic_slice(
        own_rows, ((z_lo * 2 + y_lo) * (rows // 4), z_hi * block_d), (rows // 4, block_d)
    )
    mid_part = (resid.astype(F32) + tiles.astype(F32).sum(axis=0)).astype(BF16)

    every = ("c", "yh", "x", "zh", "zl", "yl")
    moves = []
    for c in range(2):
        for d in range(n_dp):
            for z in range(n_z):
                for y in range(2):
                    source = ((c * n_dp + d) * n_z + z) * 2 + y
                    d2, g2 = c * 4 + z // 2, 4 * d + (z % 2) * 2 + y
                    c2, z2, y2 = g2 // (2 * n_z), (g2 // 2) % n_z, g2 % 2
                    moves.append((source, ((c2 * n_dp + d2) * n_z + z2) * 2 + y2))
    resid_rows = lax.ppermute(mid_part, every, moves)

    pair = to_all(resid_rows, "yl")
    mine = to_all(pair, Z).reshape(total // 2, block_d)
    theirs = lax.ppermute(mine, "c", SWAP)
    first = jnp.where(core == 0, mine, theirs)
    second = jnp.where(core == 0, theirs, mine)
    mid_cols = jnp.concatenate([first, second], axis=0)
    gain_cols = lax.dynamic_slice_in_dim(gain_mlp, block * block_d, block_d, 0).astype(F32)
    mid_f32 = mid_cols.astype(F32)
    square = jnp.sum(jnp.square(mid_f32), axis=-1)
    lhs = (mid_f32 * gain_cols[None, :]).astype(BF16)
    hidden_width = w_gate.shape[1]
    gate_up = jnp.concatenate([dot(lhs, w_gate), dot(lhs, w_up)], axis=1).astype(BF16)
    top = square.astype(BF16)
    low = (square - top.astype(F32)).astype(BF16)
    extra = jnp.concatenate([top.reshape(n_dp, 1, rows), low.reshape(n_dp, 1, rows)], axis=2)
    extra = jnp.pad(extra, ((0, 0), (0, 7), (0, 2 * hidden_width - 2 * rows)))
    tiles = jnp.concatenate([gate_up.reshape(n_dp, rows, 2 * hidden_width), extra], axis=1)
    tiles = exchange(tiles, DP).astype(F32).sum(axis=0)
    square = tiles[rows, :rows] + tiles[rows, rows : 2 * rows]
    scale = lax.rsqrt(square / (2 * half_d) + EPS)[:, None]
    gate = tiles[:rows, :hidden_width] * scale
    up = tiles[:rows, hidden_width:] * scale
    hidden = (jax.nn.silu(gate) * up).astype(BF16)

    hidden_all = to_all(hidden, DP).reshape(total, hidden_width)

    def down_half(k):
        return dot(lax.dynamic_slice_in_dim(hidden_all, k * (total // 2), total // 2, 0), w_down)

    sent = lax.ppermute(down_half(1 - core).astype(BF16), "c", SWAP)
    terms = (down_half(core) + sent.astype(F32)).astype(BF16)
    tiles = exchange(terms.reshape(n_z, total // 2 // n_z, block_d), Z)
    terms = tiles.astype(F32).sum(axis=0).astype(BF16)
    tiles = exchange(terms.reshape(2, rows // 4, block_d), "yl")
    return (resid_rows.astype(F32) + tiles.astype(F32).sum(axis=0)).astype(BF16)


def solution(mesh):
    fine = Mesh(
        mesh.devices.reshape(2, 2, 4, 4, 2, 2), ("c", "yh", "x", "zh", "zl", "yl")
    )
    placed = (
        P(DP, GROUP),
        P(),
        P(None, GROUP),
        P(None, GROUP),
        P(GROUP, None),
        P(),
        P(DP, GROUP),
        P(DP, GROUP),
        P(GROUP, DP),
    )
    return jax.shard_map(
        shards, mesh=fine, in_specs=placed, out_specs=P(GROUP, DP), check_vma=False
    )
```

time: 478 us -> 288 us (0.60)
  waiting for transfers between devices: 322 us -> 37.7 us
  blocking collectives: 71.8 us -> 180 us
  between operations: 13.4 us -> 0.39 us
  local copies, waits for them, and re-layouts: 7.15 us -> 12.8 us
    all_gather x2 -> x0, waiting for transfers between devices: 130 us -> none  [the longest x1 70.4 us: shards(): lax.all_gather(tokens_in, ('section', 'tensor'), axis=1, tiled=True)]
    all_to_all x2 -> x8, blocking collectives: 71.8 us -> 180 us  [the longest x4 101 us: exchange(): return lax.all_to_all(tiles, axis, 0, 0, tiled=True)]
    reduce_scatter x1 -> x0, waiting for transfers between devices: 84.1 us -> none  [shards(): lax.psum_scatter(jnp.concatenate([gate_block, up_block], axis=1), 'dp', s...]
    all_to_all x5 -> x3, waiting for transfers between devices: 107 us -> 22.5 us  [the longest x2 20.4 us: to_all(): lax.all_to_all(jnp.broadcast_to(array[None], (length, *array.shape)), axi...]
    all_to_all x5 -> x3, starting transfers between devices: 33.5 us -> 14 us  [the longest x2 10.6 us: to_all(): lax.all_to_all(jnp.broadcast_to(array[None], (length, *array.shape)), axi...]
    ppermute x0 -> x6, starting transfers between devices: none -> 17.6 us  [the longest x1 6.48 us: shards(): resid_rows = lax.ppermute(mid_part, every, moves)]
    ppermute x0 -> x6, waiting for transfers between devices: none -> 15.3 us  [the longest x1 6.49 us: shards(): kv_here = lax.ppermute(kv_part, GROUP, moves)]
    dot_general x8 -> x12, matrix products: 14.8 us -> 13.5 us  [the longest x11 13.1 us: dot(): return jnp.dot(a, b, preferred_element_type=F32)]
  transfers between devices with their start and end apart: 8 -> 9, of which waited for: 8 -> 9; matrix products, arithmetic and copies ran while one was open for 2% -> 4% of each run, Pallas kernels for 0% -> 0%
where the time goes in v1:
time: 288 us; the launch traced here: 287 us
  blocking collectives  180 us (62%)
  waiting for transfers between devices  37.7 us (13%)
  starting transfers between devices  31.6 us (11%)
  matrix products  13.5 us (5%)
  local copies, waits for them, and re-layouts  12.8 us (4%)
  other arithmetic  11.1 us (4%)
    all_to_all x4, blocking collectives, exchange(): return lax.all_to_all(tiles, axis, 0, 0, tiled=True)  101 us
    all_to_all x4, blocking collectives, to_all(): lax.all_to_all(jnp.broadcast_to(array[None], (length, *array.shape)), axi...  79.4 us
    all_to_all x2, waiting for transfers between devices, to_all(): lax.all_to_all(jnp.broadcast_to(array[None], (length, *array.shape)), axi...  20.4 us
    dot_general x11, matrix products, dot(): return jnp.dot(a, b, preferred_element_type=F32)  13.1 us
    all_to_all x2, starting transfers between devices, to_all(): lax.all_to_all(jnp.broadcast_to(array[None], (length, *array.shape)), axi...  10.6 us
    ppermute x1, waiting for transfers between devices, shards(): kv_here = lax.ppermute(kv_part, GROUP, moves)  6.49 us
    ppermute x1, starting transfers between devices, shards(): resid_rows = lax.ppermute(mid_part, every, moves)  6.48 us
  transfers between devices with their start and end apart: 9, of which 9 were waited for; matrix products, arithmetic and copies ran while one was open for 4% of the time, Pallas kernels for 0%

profile of v1, /device:TPU:1, one launch (start us, length us, event | category | flops | bytes accessed | tf_op | source)
XLA Modules:
  0.0 287.2 jit_solution(10865529129796338615)
XLA Ops:
  0.9 6.5 %all_to_all.55 = bf16[2,128,256]{2,1,0:T(8,128)(2,1)S(1)} all-to-all(bf16[2,128,256]{2,1,0:T(8,128)(2,1)S(1)} %broadcast_in_dim.15), channel_id=1, replica_groups=mesh['c'=2,'yh'=2,'x'=4,'zh'=4,'zl'=2,'yl'=2] {'yl'}, dimensions={0} | all-to-all | bytes 262144 | tf_op jit(solution)/shard_map/all_to_all | solution.py:27
  8.2 33.7 %all_to_all.56 = bf16[8,2,128,256]{3,1,2,0:T(2,128)(2,1)S(1)} all-to-all(bf16[8,2,128,256]{3,1,2,0:T(2,128)(2,1)S(1)} %broadcast_in_dim.16), channel_id=1, replica_groups=mesh['c'=2,'yh'=2,'x'=4,'zh'=4,'zl'=2,'yl'=2] {'zh','zl'}, dimensions={0} | all-to-all | bytes 2097152 | tf_op jit(solution)/shard_map/all_to_all | solution.py:27
  42.1 4.0 %collective-permute-start = (bf16[16,128,256]{2,1,0:T(8,128)(2,1)S(1)}, bf16[16,128,256]{2,1,0:T(8,128)(2,1)}, u32[]{:S(2)}, u32[]{:S(2)}) collective-permute-start(bf16[16,128,256]{2,1,0:T(8,128)(2,1)S(1)} %bitcast.60), channel_id=1, source_target_pairs={{0,128},{128,0},{1,129},{129,1},{2,130},{130,2},{3,131},{131,3},{4... | collective-permute-start | bytes 3145736 | tf_op jit(solution)/shard_map/ppermute | solution.py:56
  46.1 2.0 copy.60
  56.6 2.5 collective-permute-start.1
  59.1 6.5 %collective-permute-done.1 = bf16[64,128]{1,0:T(8,128)(2,1)S(1)} collective-permute-done((bf16[64,128]{1,0:T(8,128)(2,1)S(1)}, bf16[64,128]{1,0:T(8,128)(2,1)S(1)}, u32[]{:S(2)}, u32[]{:S(2)}) %collective-permute-start.1) | collective-permute-done | bytes 16416 | tf_op jit(solution)/shard_map/ppermute | solution.py:80
  66.5 7.0 %all-to-all-start.2 = ((bf16[32,64,128]{2,1,0:T(8,128)(2,1)}), bf16[32,64,128]{2,1,0:T(8,128)(2,1)S(1)}, u32[]{:S(2)}, u32[]{:S(2)}) async-start(bf16[32,64,128]{2,1,0:T(8,128)(2,1)} %broadcast_in_dim.17), calls=%async_computation.2 | async-start | bytes 1048576 | tf_op jit(solution)/shard_map/all_to_all | solution.py:27
  73.5 3.3 %fusion.12 = f32[128,256]{0,1:T(8,128)S(1)} fusion(bf16[8192,256]{1,0:T(8,128)(2,1)} %param.11, s32[]{:T(128)S(6)} %select_n.47, bf16[128,4096]{0,1:T(8,128)(2,1)} %bitcast.63, f32[4096]{0:T(1024)S(1)} %get-tuple-element.20, f32[128]{0:T(128)S(1)} %add_rsqrt_fusion), kind=kOutput, calls=%fused_computation.21 | convolution fusion | flops 270532608 | bytes 3293700 | tf_op jit(solution)/shard_map/dot_general | solution.py:22
  76.8 2.4 fusion.25
  79.5 3.1 %all-to-all-done.2 = bf16[32,64,128]{2,1,0:T(8,128)(2,1)S(1)} async-done(((bf16[32,64,128]{2,1,0:T(8,128)(2,1)}), bf16[32,64,128]{2,1,0:T(8,128)(2,1)S(1)}, u32[]{:S(2)}, u32[]{:S(2)}) %all-to-all-start.2) | async-done | bytes 524320 | tf_op jit(solution)/shard_map/all_to_all | solution.py:27
  87.5 2.6 collective-permute-done.2
  91.8 30.7 %all_to_all.57 = bf16[8,64,1024]{2,1,0:T(8,128)(2,1)S(1)} all-to-all(bf16[8,64,1024]{2,1,0:T(8,128)(2,1)S(1)} %bitcast.61), channel_id=1, replica_groups=mesh['c'=2,'yh'=2,'x'=4,'zh'=4,'zl'=2,'yl'=2] {'zh','zl'}, dimensions={0} | all-to-all | bytes 2097152 | tf_op jit(solution)/shard_map/all_to_all | solution.py:33
  123.3 3.4 %all-to-all-start.4 = ((bf16[2,32,1024]{2,1,0:T(8,128)(2,1)}), bf16[2,32,1024]{2,1,0:T(8,128)(2,1)S(1)}, u32[]{:S(2)}, u32[]{:S(2)}) async-start(bf16[2,32,1024]{2,1,0:T(8,128)(2,1)} %bitcast.18), calls=%async_computation.4 | async-start | bytes 262144 | tf_op jit(solution)/shard_map/all_to_all | solution.py:33
  128.0 2.1 all-to-all-done.4
  130.1 6.5 %collective-permute-start.3 = (bf16[32,1024]{1,0:T(8,128)(2,1)S(1)}, bf16[32,1024]{1,0:T(8,128)(2,1)S(1)}, u32[]{:S(2)}, u32[]{:S(2)}) collective-permute-start(bf16[32,1024]{1,0:T(8,128)(2,1)S(1)} %add_convert_fusion.3), channel_id=1, source_target_pairs={{0,0},{1,1},{2,2},{3,3},{4,16},{5,17},{6,18},{7,19},{8,32},{9,33},... | collective-permute-start | bytes 196616 | tf_op jit(solution)/shard_map/ppermute | solution.py:140
  138.5 5.7 %all_to_all.58 = bf16[2,32,1024]{2,1,0:T(8,128)(2,1)S(1)} all-to-all(bf16[2,32,1024]{2,1,0:T(8,128)(2,1)S(1)} %broadcast_in_dim.19), channel_id=1, replica_groups=mesh['c'=2,'yh'=2,'x'=4,'zh'=4,'zl'=2,'yl'=2] {'yl'}, dimensions={0} | all-to-all | bytes 262144 | tf_op jit(solution)/shard_map/all_to_all | solution.py:27
  144.3 33.4 %all_to_all.59 = bf16[8,2,32,1024]{3,2,1,0:T(8,128)(2,1)S(1)} all-to-all(bf16[8,2,32,1024]{3,2,1,0:T(8,128)(2,1)S(1)} %broadcast_in_dim.20), channel_id=1, replica_groups=mesh['c'=2,'yh'=2,'x'=4,'zh'=4,'zl'=2,'yl'=2] {'zh','zl'}, dimensions={0} | all-to-all | bytes 2097152 | tf_op jit(solution)/shard_map/all_to_all | solution.py:27
  177.8 3.8 %collective-permute-start.4 = (bf16[512,1024]{1,0:T(8,128)(2,1)S(1)}, bf16[512,1024]{1,0:T(8,128)(2,1)S(1)}, u32[]{:S(2)}, u32[]{:S(2)}) collective-permute-start(bf16[512,1024]{1,0:T(8,128)(2,1)S(1)} %bitcast.59), channel_id=1, source_target_pairs={{0,128},{128,0},{1,129},{129,1},{2,130},{130,2},{3,131},{131,3},{4... | collective-permute-start | bytes 3145736 | tf_op jit(solution)/shard_map/ppermute | solution.py:144
  188.2 32.6 %all_to_all.60 = bf16[8,136,1024]{2,1,0:T(8,128)(2,1)S(1)} all-to-all(bf16[8,136,1024]{2,1,0:T(8,128)(2,1)S(1)} %pad_maximum_fusion), channel_id=1, replica_groups=mesh['c'=2,'yh'=2,'x'=4,'zh'=4,'zl'=2,'yl'=2] {'yh','x'}, dimensions={0} | all-to-all | bytes 4456448 | tf_op jit(solution)/shard_map/all_to_all | solution.py:33
  222.4 3.6 %all-to-all-start.8 = ((bf16[8,128,512]{2,1,0:T(8,128)(2,1)}), bf16[8,128,512]{2,1,0:T(8,128)(2,1)S(1)}, u32[]{:S(2)}, u32[]{:S(2)}) async-start(bf16[8,128,512]{2,1,0:T(8,128)(2,1)} %broadcast_in_dim.21), calls=%async_computation.8 | async-start | bytes 2097152 | tf_op jit(solution)/shard_map/all_to_all | solution.py:27
  226.0 17.3 %all-to-all-done.8 = bf16[8,128,512]{2,1,0:T(8,128)(2,1)S(1)} async-done(((bf16[8,128,512]{2,1,0:T(8,128)(2,1)}), bf16[8,128,512]{2,1,0:T(8,128)(2,1)S(1)}, u32[]{:S(2)}, u32[]{:S(2)}) %all-to-all-start.8) | async-done | bytes 1048608 | tf_op jit(solution)/shard_map/all_to_all | solution.py:27
  245.8 2.5 collective-permute-done.5
  249.0 31.6 %all_to_all.61 = bf16[8,64,1024]{2,1,0:T(8,128)(2,1)S(1)} all-to-all(bf16[8,64,1024]{2,1,0:T(8,128)(2,1)S(1)} %bitcast.70), channel_id=1, replica_groups=mesh['c'=2,'yh'=2,'x'=4,'zh'=4,'zl'=2,'yl'=2] {'zh','zl'}, dimensions={0} | all-to-all | bytes 2097152 | tf_op jit(solution)/shard_map/all_to_all | solution.py:33
  280.8 5.7 %all_to_all.62 = bf16[2,32,1024]{2,1,0:T(8,128)(2,1)S(1)} all-to-all(bf16[2,32,1024]{2,1,0:T(8,128)(2,1)S(1)} %bitcast.71), channel_id=1, replica_groups=mesh['c'=2,'yh'=2,'x'=4,'zh'=4,'zl'=2,'yl'=2] {'yl'}, dimensions={0} | all-to-all | bytes 262144 | tf_op jit(solution)/shard_map/all_to_all | solution.py:33
  (75 shorter events, 34.3 us)
Async XLA Ops:
  0.0 243.3 %copy-start = (bf16[512,1024]{1,0:T(8,128)(2,1)S(1)}, bf16[512,1024]{1,0:T(8,128)(2,1)}, u32[]{:S(2)}) copy-start(bf16[512,1024]{1,0:T(8,128)(2,1)} %param.17) | copy-start | bytes 3145732
  8.1 38.0 %copy-start.4 = (bf16[8192]{0:T(1024)(128)(2,1)S(1)}, bf16[8192]{0:T(1024)(128)(2,1)}, u32[]{:S(2)}) copy-start(bf16[8192]{0:T(1024)(128)(2,1)} %param.10) | copy-start | bytes 49156
  42.1 6.4 %collective-permute-start = (bf16[16,128,256]{2,1,0:T(8,128)(2,1)S(1)}, bf16[16,128,256]{2,1,0:T(8,128)(2,1)}, u32[]{:S(2)}, u32[]{:S(2)}) collective-permute-start(bf16[16,128,256]{2,1,0:T(8,128)(2,1)S(1)} %bitcast.60), channel_id=1, source_target_pairs={{0,128},{128,0},{1,129},{129,1},{2,130},{130,2},{3,131},{131,3},{4... | collective-permute-start | bytes 3145736 | tf_op jit(solution)/shard_map/ppermute | solution.py:56
  51.8 3.6 %copy-start.2 = (bf16[8,2,128,256]{2,3,1,0:T(8,128)(2,1)S(1)}, bf16[8,2,128,256]{2,3,1,0:T(8,128)(2,1)}, u32[]{:S(2)}) copy-start(bf16[8,2,128,256]{2,3,1,0:T(8,128)(2,1)} %copy.60) | copy-start | bytes 3145732
  51.8 3.6 %copy-start.3 = (bf16[8192,64]{0,1:T(8,128)(2,1)S(1)}, bf16[8192,64]{0,1:T(8,128)(2,1)}, u32[]{:S(2)}) copy-start(bf16[8192,64]{0,1:T(8,128)(2,1)} %param.12) | copy-start | bytes 3145732
  56.6 9.0 %collective-permute-start.1 = (bf16[64,128]{1,0:T(8,128)(2,1)S(1)}, bf16[64,128]{1,0:T(8,128)(2,1)S(1)}, u32[]{:S(2)}, u32[]{:S(2)}) collective-permute-start(bf16[64,128]{1,0:T(8,128)(2,1)S(1)} %fusion.28), channel_id=1, source_target_pairs={{0,0},{1,1},{2,4},{3,5},{4,8},{5,9},{6,12},{7,13},{8,128},{9,129},... | collective-permute-start | bytes 49160 | tf_op jit(solution)/shard_map/ppermute | solution.py:80
  66.5 16.1 %all-to-all-start.2 = ((bf16[32,64,128]{2,1,0:T(8,128)(2,1)}), bf16[32,64,128]{2,1,0:T(8,128)(2,1)S(1)}, u32[]{:S(2)}, u32[]{:S(2)}) async-start(bf16[32,64,128]{2,1,0:T(8,128)(2,1)} %broadcast_in_dim.17), calls=%async_computation.2 | async-start | bytes 1048576 | tf_op jit(solution)/shard_map/all_to_all | solution.py:27
  84.8 2.2 copy-start.1
  87.4 2.7 collective-permute-start.2
  123.3 6.7 %all-to-all-start.4 = ((bf16[2,32,1024]{2,1,0:T(8,128)(2,1)}), bf16[2,32,1024]{2,1,0:T(8,128)(2,1)S(1)}, u32[]{:S(2)}, u32[]{:S(2)}) async-start(bf16[2,32,1024]{2,1,0:T(8,128)(2,1)} %bitcast.18), calls=%async_computation.4 | async-start | bytes 262144 | tf_op jit(solution)/shard_map/all_to_all | solution.py:33
  130.1 8.4 %collective-permute-start.3 = (bf16[32,1024]{1,0:T(8,128)(2,1)S(1)}, bf16[32,1024]{1,0:T(8,128)(2,1)S(1)}, u32[]{:S(2)}, u32[]{:S(2)}) collective-permute-start(bf16[32,1024]{1,0:T(8,128)(2,1)S(1)} %add_convert_fusion.3), channel_id=1, source_target_pairs={{0,0},{1,1},{2,2},{3,3},{4,16},{5,17},{6,18},{7,19},{8,32},{9,33},... | collective-permute-start | bytes 196616 | tf_op jit(solution)/shard_map/ppermute | solution.py:140
  177.8 6.1 %collective-permute-start.4 = (bf16[512,1024]{1,0:T(8,128)(2,1)S(1)}, bf16[512,1024]{1,0:T(8,128)(2,1)S(1)}, u32[]{:S(2)}, u32[]{:S(2)}) collective-permute-start(bf16[512,1024]{1,0:T(8,128)(2,1)S(1)} %bitcast.59), channel_id=1, source_target_pairs={{0,128},{128,0},{1,129},{129,1},{2,130},{130,2},{3,131},{131,3},{4... | collective-permute-start | bytes 3145736 | tf_op jit(solution)/shard_map/ppermute | solution.py:144
  184.0 1.2 copy-start.5
  185.3 1.3 copy-start.6
  222.4 20.9 %all-to-all-start.8 = ((bf16[8,128,512]{2,1,0:T(8,128)(2,1)}), bf16[8,128,512]{2,1,0:T(8,128)(2,1)S(1)}, u32[]{:S(2)}, u32[]{:S(2)}) async-start(bf16[8,128,512]{2,1,0:T(8,128)(2,1)} %broadcast_in_dim.21), calls=%async_computation.8 | async-start | bytes 2097152 | tf_op jit(solution)/shard_map/all_to_all | solution.py:27
  245.0 3.3 %collective-permute-start.5 = (bf16[512,1024]{1,0:T(8,128)(2,1)}, bf16[512,1024]{1,0:T(8,128)(2,1)S(1)}, u32[]{:S(2)}, u32[]{:S(2)}) collective-permute-start(bf16[512,1024]{1,0:T(8,128)(2,1)} %convolution_convert_fusion.1), channel_id=1, source_target_pairs={{0,128},{128,0},{1,129},{129,1},{2,130},{130,2},{3,131},{131,3},{4... | collective-permute-start | bytes 3145736 | tf_op jit(solution)/shard_map/ppermute | solution.py:171
